TPU v7x, 32 devices: a whole 2x2x4 slice. The times are simulated.
32 devices in a mesh: rows: 8 (over z, x), cols: 4 (over y, core).
Axes of the slice: x: 2, y: 2, z: 4, core: 2. Of those that a mesh axis runs over, the one named last changes fastest.
Arguments:
- panel_t: float32 [16, 2048], P(None, ('rows', 'cols')), may hold values from -6 to 6
- kinship: float32 [2048, 2048], P('rows', 'cols'), may hold values from -0.125 to 0.125
Outputs:
- kin_panel_t: float32 [16, 2048], P(None, ('rows', 'cols'))
- score: float32 [16, 16], replicated
All inputs are finite; a program needn't handle non-finite values.
Results may differ from a plain program's by a relative error of at most 0.00008.
Values sent between devices are 32-bit elements; how exact they have to be, the bound alone decides.
A program may use at most 64 MiB of HBM per device.

v0:
```python
import functools
import math

import jax
import jax.numpy as jnp
from jax import lax
from jax.experimental import pallas as pl
from jax.experimental.pallas import tpu as pltpu
from jax.sharding import PartitionSpec as P

MESH = pl.DeviceIdType.MESH
LANES = 128
SUBLANES = 8


def split(x):
    high = x.astype(jnp.bfloat16)
    rest = x - high.astype(jnp.float32)
    mid = rest.astype(jnp.bfloat16)
    low = (rest - mid.astype(jnp.float32)).astype(jnp.bfloat16)
    return high, mid, low


def dot(left, right, dims):
    n = left[0].shape[0]

    def one(pieces, weights):
        return lax.dot_general(
            jnp.concatenate(pieces, axis=0),
            weights,
            (dims, ((), ())),
            preferred_element_type=jnp.float32,
        )

    high, mid, low = one(left, right[0]), one(left[:2], right[1]), one(left[:1], right[2])
    small = high[2 * n :] + mid[n:] + low
    return high[:n] + (high[n : 2 * n] + mid[:n] + small)


def fold(x):
    half = x.shape[0] // 2
    return jnp.concatenate([x[:half], x[half:]], axis=1)


def unfold(x):
    own = x.shape[1] // 2
    return jnp.concatenate([x[:, :own], x[:, own:]], axis=0)


def join(chunks):
    own = chunks[0].shape[1] // 2
    return jnp.concatenate(
        [
            jnp.concatenate([x[:, :own] for x in chunks], axis=1),
            jnp.concatenate([x[:, own:] for x in chunks], axis=1),
        ],
        axis=0,
    )


def remote(src, dst, send, recv, where):
    return pltpu.make_async_remote_copy(
        src_ref=src,
        dst_ref=dst,
        send_sem=send,
        recv_sem=recv,
        device_id=where,
        device_id_type=MESH,
    )


def kernel(
    rows,
    cols,
    panel_hbm,
    kin_hbm,
    out_ref,
    score_ref,
    loaded,
    panel,
    kin,
    kin_high,
    kin_mid,
    kin_low,
    slab,
    block,
    part,
    landed,
    forms,
    panel_sem,
    kin_sem,
    slab_send,
    slab_recv,
    block_send,
    block_recv,
    part_send,
    part_recv,
    forms_send,
    forms_recv,
):
    count = rows * cols
    depth = rows // cols
    plane = depth * cols
    traits, own = panel_hbm.shape
    row, col = lax.axis_index("rows"), lax.axis_index("cols")
    me = row * cols + col
    zz = row // depth
    mine = me % plane

    def others(body):
        back = zz < cols // 2
        peers = [(col + step) % cols for step in range(cols)]

        def row_of(step, carry):
            r = jnp.where(back, row - step, row + step)
            r = jnp.where(r < 0, r + rows, jnp.where(r >= rows, r - rows, r))
            for c in peers:
                body((r, c))
            return carry

        lax.fori_loop(1, rows, row_of, 0)
        for c in peers[1:]:
            body((row, c))

    barrier = pltpu.get_barrier_semaphore()
    others(
        lambda where: pl.semaphore_signal(
            barrier, inc=1, device_id=where, device_id_type=MESH
        )
    )
    get_panel = pltpu.make_async_copy(panel_hbm, loaded, panel_sem)
    get_panel.start()
    get_kin = pltpu.make_async_copy(kin_hbm, kin, kin_sem)
    get_kin.start()
    get_panel.wait()
    panel[...] = fold(loaded[...])
    slab[col] = panel[...]
    pl.semaphore_wait(barrier, count - 1)

    for step in range(1, cols):
        c = (col + step) % cols
        remote(panel, slab.at[col], slab_send, slab_recv, (row, c)).start()

    keep_block = pltpu.make_async_copy(panel, block.at[mine], block_recv)
    send_block = remote(panel, block.at[mine], block_send, block_recv, (row, zz))
    sign = jnp.where(zz < cols // 2, rows - 1, 1)
    for step in range(1, rows):
        r = (row + sign * step) % rows
        remote(panel, block.at[mine], block_send, block_recv, (r, zz)).start()

    @pl.when(col == zz)
    def _():
        keep_block.start()

    @pl.when(col != zz)
    def _():
        send_block.start()

    def wait_bytes(ref, sem):
        pltpu.make_async_copy(ref, ref, sem).wait()

    get_kin.wait()
    kin_high[...], kin_mid[...], kin_low[...] = split(kin[...])
    wait_bytes(slab.at[pl.ds(0, cols - 1)], slab_recv)
    weights = (kin_high[...], kin_mid[...], kin_low[...])
    slab_panel = join([slab[c] for c in range(cols)])
    side = dot(split(slab_panel / math.sqrt(count * own)), weights, ((1,), (0,)))
    wide = tuple(jnp.concatenate([x] * (LANES // traits), axis=0) for x in split(side))

    wait_bytes(block, block_recv)
    block_panel = split(join([block[m] for m in range(plane)]))
    spread = dot(block_panel, wide, ((1,), (1,)))
    sublane = lax.broadcasted_iota(jnp.int32, (traits, LANES), 0) % SUBLANES
    group = lax.broadcasted_iota(jnp.int32, (traits, LANES), 1) // traits
    spread = jnp.where(sublane == group, spread, 0.0)
    forms[me] = jnp.sum(spread.reshape(traits // SUBLANES, SUBLANES, LANES), axis=1)
    others(
        lambda where: remote(
            forms.at[me], forms.at[me], forms_send, forms_recv, where
        ).start()
    )

    value = dot(block_panel, (kin_high[...], kin_mid[...], kin_low[...]), ((1,), (1,)))
    for c in range(cols):
        part[c] = fold(value[:, c * own : (c + 1) * own])
    for step in range(1, cols):
        c = (col + step) % cols
        remote(part.at[c], landed.at[col], part_send, part_recv, (row, c)).start()
    landed[col] = part[col]

    wait_bytes(landed.at[pl.ds(0, cols - 1)], part_recv)
    result = landed[0]
    for c in range(1, cols):
        result += landed[c]
    out_ref[...] = unfold(result)

    wait_bytes(block.at[pl.ds(0, rows - 1)], block_send)

    @pl.when(col != zz)
    def _():
        send_block.wait_send()

    wait_bytes(slab.at[pl.ds(0, cols - 1)], slab_send)
    wait_bytes(landed.at[pl.ds(0, cols - 1)], part_send)
    wait_bytes(forms.at[pl.ds(0, count - 1)], forms_send)
    wait_bytes(forms.at[pl.ds(0, count - 1)], forms_recv)
    total = jnp.sum(forms[...], axis=0)
    spread = jnp.concatenate(
        [
            jnp.broadcast_to(total[i : i + 1, :], (SUBLANES, LANES))
            for i in range(traits // SUBLANES)
        ],
        axis=0,
    )
    spread = jnp.where(sublane == group, spread, 0.0)
    score_ref[...] = jnp.sum(spread.T.reshape(LANES // traits, traits, traits), axis=0)


def finish(value_ref, form_ref, out_ref, score_ref, sems):
    first = pltpu.make_async_copy(value_ref, out_ref, sems.at[0])
    second = pltpu.make_async_copy(form_ref, score_ref, sems.at[1])
    first.start()
    second.start()
    first.wait()
    second.wait()


def shards(rows, cols, panel_t, kinship):
    traits, own = panel_t.shape
    plane = rows // cols * cols
    vmem = pltpu.VMEM
    dma = pltpu.SemaphoreType.DMA
    f32, bf16 = jnp.float32, jnp.bfloat16
    chunk = (traits // 2, 2 * own)
    value, score = (
        pl.pallas_call(
            functools.partial(kernel, rows, cols),
            out_shape=(vmem((traits, own), f32), vmem((traits, traits), f32)),
            in_specs=[pl.BlockSpec(memory_space=pl.ANY)] * 2,
            out_specs=(pl.BlockSpec(memory_space=vmem),) * 2,
            scratch_shapes=[
                vmem((traits, own), f32),
                vmem(chunk, f32),
                vmem(kinship.shape, f32),
                vmem(kinship.shape, bf16),
                vmem(kinship.shape, bf16),
                vmem(kinship.shape, bf16),
                vmem((cols,) + chunk, f32),
                vmem((plane,) + chunk, f32),
                vmem((cols,) + chunk, f32),
                vmem((cols,) + chunk, f32),
                vmem((rows * cols, traits * traits // LANES, LANES), f32),
            ]
            + [dma(())] * 10,
            compiler_params=pltpu.CompilerParams(collective_id=0, has_side_effects=True),
        )(panel_t, kinship)
    )
    return tuple(
        pl.pallas_call(
            finish,
            out_shape=(
                jax.ShapeDtypeStruct((traits, own), f32),
                jax.ShapeDtypeStruct((traits, traits), f32),
            ),
            in_specs=[pl.BlockSpec(memory_space=pl.ANY)] * 2,
            out_specs=(pl.BlockSpec(memory_space=pl.ANY),) * 2,
            scratch_shapes=[dma((2,))],
            compiler_params=pltpu.CompilerParams(vmem_limit_bytes=1024 * 1024),
        )(value, score)
    )


def solution(mesh):
    rows, cols = mesh.shape["rows"], mesh.shape["cols"]
    return jax.shard_map(
        functools.partial(shards, rows, cols),
        mesh=mesh,
        in_specs=(P(None, ("rows", "cols")), P("rows", "cols")),
        out_specs=(P(None, ("rows", "cols")), P()),
        check_vma=False,
    )
```

profile of v0, /device:TPU:0, one launch (start us, length us, event | category | flops | bytes accessed | tf_op | source)
XLA Modules:
  0.0 16.7 jit_solution(5127114484347094513)
XLA Ops:
  0.6 15.5 %shard_map.41 = (f32[16,64]{1,0:T(8,128)S(1)}, f32[16,16]{1,0:T(8,128)S(1)}) custom-call(f32[16,64]{1,0:T(8,128)} %panel_hbm.1, f32[256,512]{1,0:T(8,128)} %kin_hbm.1), custom_call_target="tpu_custom_call" | custom-call | tf_op jit(solution)/shard_map/pallas_call | solution.py:236
  16.1 0.6 %shard_map.42 = (f32[16,64]{1,0:T(8,128)}, f32[16,16]{1,0:T(8,128)}) custom-call(f32[16,64]{1,0:T(8,128)S(1)} %get-tuple-element.4.value_ref, f32[16,16]{1,0:T(8,128)S(1)} %get-tuple-element.5.form_ref), custom_call_target="tpu_custom_call" | custom-call | tf_op jit(solution)/shard_map/pallas_call | solution.py:259
where the time goes:
time: 16.9 us; the launch traced here: 16.7 us
  Pallas kernels  16.1 us (95%)
  between operations  0.64 us (4%)
    pallas_call x1, Pallas kernels, shards(): pl.pallas_call(functools.partial(kernel, rows, cols), out_shape=(vmem((tr...  15.5 us
    pallas_call x1, Pallas kernels, shards(): pl.pallas_call(finish, out_shape=(jax.ShapeDtypeStruct((traits, own), f32...  0.62 us

commit v1 on v0

--- a/solution.py
+++ b/solution.py
@@ -86,17 +86,30 @@
     block,
     part,
     landed,
+    side,
+    sides,
+    samples,
+    form,
     forms,
+    total,
     panel_sem,
     kin_sem,
     slab_send,
     slab_recv,
     block_send,
     block_recv,
+    relay_send,
     part_send,
     part_recv,
-    forms_send,
+    side_send,
+    side_recv,
+    sample_send,
+    sample_recv,
+    form_send,
     forms_recv,
+    last_send,
+    total_send,
+    total_recv,
 ):
     count = rows * cols
     depth = rows // cols
@@ -104,30 +117,58 @@
     traits, own = panel_hbm.shape
     row, col = lax.axis_index("rows"), lax.axis_index("cols")
     me = row * cols + col
-    zz = row // depth
+    zz, xx = row // depth, row % depth
     mine = me % plane
 
-    def others(body):
-        back = zz < cols // 2
-        peers = [(col + step) % cols for step in range(cols)]
-
-        def row_of(step, carry):
-            r = jnp.where(back, row - step, row + step)
-            r = jnp.where(r < 0, r + rows, jnp.where(r >= rows, r - rows, r))
-            for c in peers:
-                body((r, c))
+    late = zz > col
+    early = zz <= col
+    diagonal = zz == col
+    first = (row == 0) & (col == 0)
+    root = (row == 0) & (col == 1)
+    n_early = depth * (cols * (cols + 1) // 2)
+    starts = [depth * (c * (cols - 1) - c * (c - 1) // 2) for c in range(cols)]
+    early_slot = (col * (col + 1) // 2 + zz) * depth + xx
+    late_slot = depth * (col * (cols - 1) - col * (col - 1) // 2 + zz - col - 1) + xx
+    to_first, to_root = (0, 0), (0, 1)
+
+    barrier = pltpu.get_barrier_semaphore()
+
+    def greet(where):
+        pl.semaphore_signal(barrier, inc=1, device_id=where, device_id_type=MESH)
+
+    def each_row(low, high, body):
+        def step(r, carry):
+            body(r)
             return carry
 
-        lax.fori_loop(1, rows, row_of, 0)
-        for c in peers[1:]:
-            body((row, c))
-
-    barrier = pltpu.get_barrier_semaphore()
-    others(
-        lambda where: pl.semaphore_signal(
-            barrier, inc=1, device_id=where, device_id_type=MESH
-        )
-    )
+        lax.fori_loop(low, high, step, 0)
+
+    for step in range(1, cols):
+        greet((row, (col + step) % cols))
+
+    @pl.when(late)
+    def _():
+        greet((col * depth + xx, col))
+
+    @pl.when(early)
+    def _():
+        def body(r):
+            for c in range(cols):
+
+                @pl.when((r != row) | (col != c))
+                def _():
+                    greet((r, c))
+
+        each_row(col * depth, col * depth + depth, body)
+
+    @pl.when(first | root)
+    def _():
+        def body(r):
+            for c in range(cols):
+                greet((r, c))
+
+        each_row(1, rows, body)
+
     get_panel = pltpu.make_async_copy(panel_hbm, loaded, panel_sem)
     get_panel.start()
     get_kin = pltpu.make_async_copy(kin_hbm, kin, kin_sem)
@@ -135,26 +176,39 @@
     get_panel.wait()
     panel[...] = fold(loaded[...])
     slab[col] = panel[...]
-    pl.semaphore_wait(barrier, count - 1)
+    pl.semaphore_wait(
+        barrier,
+        (cols - 1)
+        + (zz + 1) * depth
+        + jnp.where(diagonal, cols - 2 - zz, 0)
+        + jnp.where(row > 0, 2, 0),
+    )
 
     for step in range(1, cols):
         c = (col + step) % cols
         remote(panel, slab.at[col], slab_send, slab_recv, (row, c)).start()
 
+    def to_block(r):
+        @pl.when((r != row) | (col != zz))
+        def _():
+            remote(panel, block.at[mine], block_send, block_recv, (r, zz)).start()
+
+    each_row(0, zz * depth + depth, to_block)
     keep_block = pltpu.make_async_copy(panel, block.at[mine], block_recv)
-    send_block = remote(panel, block.at[mine], block_send, block_recv, (row, zz))
-    sign = jnp.where(zz < cols // 2, rows - 1, 1)
-    for step in range(1, rows):
-        r = (row + sign * step) % rows
-        remote(panel, block.at[mine], block_send, block_recv, (r, zz)).start()
-
-    @pl.when(col == zz)
+    send_sample = remote(panel, samples.at[me], sample_send, sample_recv, to_root)
+    sampled = (zz < cols - 1) & ((row != 0) | (col != 1))
+
+    @pl.when(diagonal)
     def _():
         keep_block.start()
 
-    @pl.when(col != zz)
-    def _():
-        send_block.start()
+    @pl.when(sampled)
+    def _():
+        send_sample.start()
+
+    @pl.when(root)
+    def _():
+        samples[1] = panel[...]
 
     def wait_bytes(ref, sem):
         pltpu.make_async_copy(ref, ref, sem).wait()
@@ -164,21 +218,57 @@
     wait_bytes(slab.at[pl.ds(0, cols - 1)], slab_recv)
     weights = (kin_high[...], kin_mid[...], kin_low[...])
     slab_panel = join([slab[c] for c in range(cols)])
-    side = dot(split(slab_panel / math.sqrt(count * own)), weights, ((1,), (0,)))
-    wide = tuple(jnp.concatenate([x] * (LANES // traits), axis=0) for x in split(side))
-
+    value = dot(split(slab_panel / math.sqrt(count * own)), weights, ((1,), (0,)))
+    side[...] = value
+    send_side = remote(
+        side, sides.at[late_slot], side_send, side_recv.at[col], to_root
+    )
+
+    @pl.when(late)
+    def _():
+        send_side.start()
+
+    def widen(x):
+        return tuple(jnp.concatenate([p] * (LANES // traits), axis=0) for p in split(x))
+
+    sublane = lax.broadcasted_iota(jnp.int32, (traits, LANES), 0) % SUBLANES
+    group = lax.broadcasted_iota(jnp.int32, (traits, LANES), 1) // traits
+
+    def form_of(panels, wide):
+        spread = dot(panels, wide, ((1,), (1,)))
+        spread = jnp.where(sublane == group, spread, 0.0)
+        return jnp.sum(spread.reshape(traits // SUBLANES, SUBLANES, LANES), axis=1)
+
+    wide = widen(value)
     wait_bytes(block, block_recv)
     block_panel = split(join([block[m] for m in range(plane)]))
-    spread = dot(block_panel, wide, ((1,), (1,)))
-    sublane = lax.broadcasted_iota(jnp.int32, (traits, LANES), 0) % SUBLANES
-    group = lax.broadcasted_iota(jnp.int32, (traits, LANES), 1) // traits
-    spread = jnp.where(sublane == group, spread, 0.0)
-    forms[me] = jnp.sum(spread.reshape(traits // SUBLANES, SUBLANES, LANES), axis=1)
-    others(
-        lambda where: remote(
-            forms.at[me], forms.at[me], forms_send, forms_recv, where
-        ).start()
-    )
+    form[...] = form_of(block_panel, wide)
+    form_first = remote(form, forms.at[early_slot], form_send, forms_recv, to_first)
+    form_root = remote(form, forms.at[early_slot], form_send, forms_recv, to_root)
+
+    @pl.when(early & ((row != 0) | (col != 0)))
+    def _():
+        form_first.start()
+
+    @pl.when(early & ((row != 0) | (col != 1)))
+    def _():
+        form_root.start()
+
+    @pl.when(first)
+    def _():
+        forms[0] = form[...]
+
+    @pl.when(root)
+    def _():
+        forms[depth] = form[...]
+
+    @pl.when(diagonal)
+    def _():
+        def relay(z):
+            where = (z * depth + xx, col)
+            remote(block, block, relay_send, block_recv, where).start()
+
+        each_row(zz + 1, cols, relay)
 
     value = dot(block_panel, (kin_high[...], kin_mid[...], kin_low[...]), ((1,), (1,)))
     for c in range(cols):
@@ -188,26 +278,92 @@
         remote(part.at[c], landed.at[col], part_send, part_recv, (row, c)).start()
     landed[col] = part[col]
 
+    send_last = remote(
+        forms.at[n_early], forms.at[n_early], last_send, forms_recv, to_first
+    )
+
+    def to_all(r):
+        for c in range(cols):
+
+            @pl.when((r != 0) | (c > 1))
+            def _():
+                remote(total, total, total_send, total_recv, (r, c)).start()
+
+    @pl.when(root)
+    def _():
+        wait_bytes(samples.at[pl.ds(0, plane * (cols - 1) - 1)], sample_recv)
+        last = jnp.zeros((traits // SUBLANES, LANES), jnp.float32)
+        for c in range(cols - 1):
+            low, n = starts[c], starts[c + 1] - starts[c]
+            panels = split(join([samples[c * plane + m] for m in range(plane)]))
+            wait_bytes(sides.at[pl.ds(low, n)], side_recv.at[c])
+            last += form_of(panels, widen(jnp.sum(sides[low : low + n], axis=0)))
+        forms[n_early] = last
+        send_last.start()
+        wait_bytes(forms.at[pl.ds(0, n_early - 1)], forms_recv)
+        total[...] = jnp.sum(forms[...], axis=0)
+        each_row(0, rows, to_all)
+
     wait_bytes(landed.at[pl.ds(0, cols - 1)], part_recv)
     result = landed[0]
     for c in range(1, cols):
         result += landed[c]
     out_ref[...] = unfold(result)
 
-    wait_bytes(block.at[pl.ds(0, rows - 1)], block_send)
-
-    @pl.when(col != zz)
-    def _():
-        send_block.wait_send()
-
     wait_bytes(slab.at[pl.ds(0, cols - 1)], slab_send)
+    for z in range(cols):
+
+        @pl.when((zz == z) & (col != z))
+        def _():
+            wait_bytes(block.at[pl.ds(0, (z + 1) * depth)], block_send)
+
+        @pl.when((zz == z) & (col == z))
+        def _():
+            if (z + 1) * depth > 1:
+                wait_bytes(block.at[pl.ds(0, (z + 1) * depth - 1)], block_send)
+
+    @pl.when(diagonal)
+    def _():
+        each_row(zz + 1, cols, lambda z: wait_bytes(block, relay_send))
+
+    @pl.when(sampled)
+    def _():
+        send_sample.wait_send()
+
+    @pl.when(late)
+    def _():
+        send_side.wait_send()
+
+    @pl.when(early & ((row != 0) | (col != 0)))
+    def _():
+        form_first.wait_send()
+
+    @pl.when(early & ((row != 0) | (col != 1)))
+    def _():
+        form_root.wait_send()
+
     wait_bytes(landed.at[pl.ds(0, cols - 1)], part_send)
-    wait_bytes(forms.at[pl.ds(0, count - 1)], forms_send)
-    wait_bytes(forms.at[pl.ds(0, count - 1)], forms_recv)
-    total = jnp.sum(forms[...], axis=0)
+
+    @pl.when(root)
+    def _():
+        send_last.wait_send()
+        for _ in range(cols - 2):
+            wait_bytes(total, total_send)
+        each_row(0, (rows - 1) * cols, lambda r: wait_bytes(total, total_send))
+
+    @pl.when(first)
+    def _():
+        wait_bytes(forms.at[pl.ds(0, n_early)], forms_recv)
+        total[...] = jnp.sum(forms[...], axis=0)
+
+    @pl.when((row != 0) | (col > 1))
+    def _():
+        wait_bytes(total, total_recv)
+
+    whole = total[...]
     spread = jnp.concatenate(
         [
-            jnp.broadcast_to(total[i : i + 1, :], (SUBLANES, LANES))
+            jnp.broadcast_to(whole[i : i + 1, :], (SUBLANES, LANES))
             for i in range(traits // SUBLANES)
         ],
         axis=0,
@@ -232,6 +388,9 @@
     dma = pltpu.SemaphoreType.DMA
     f32, bf16 = jnp.float32, jnp.bfloat16
     chunk = (traits // 2, 2 * own)
+    form = (traits * traits // LANES, LANES)
+    n_early = plane * (cols + 1) // 2
+    n_late = plane * (cols - 1) // 2
     value, score = (
         pl.pallas_call(
             functools.partial(kernel, rows, cols),
@@ -249,9 +408,16 @@
                 vmem((plane,) + chunk, f32),
                 vmem((cols,) + chunk, f32),
                 vmem((cols,) + chunk, f32),
-                vmem((rows * cols, traits * traits // LANES, LANES), f32),
+                vmem((traits, kinship.shape[1]), f32),
+                vmem((n_late, traits, kinship.shape[1]), f32),
+                vmem((plane * (cols - 1),) + chunk, f32),
+                vmem(form, f32),
+                vmem((n_early + 1,) + form, f32),
+                vmem(form, f32),
             ]
-            + [dma(())] * 10,
+            + [dma(())] * 10
+            + [dma((cols,))]
+            + [dma(())] * 7,
             compiler_params=pltpu.CompilerParams(collective_id=0, has_side_effects=True),
         )(panel_t, kinship)
     )

time: 16.9 us -> 15.9 us (0.941)
  Pallas kernels: 16.1 us -> 15 us
    pallas_call x1, Pallas kernels: 15.5 us -> 14.4 us  [shards(): pl.pallas_call(functools.partial(kernel, rows, cols), out_shape=(vmem((tr...]
where the time goes in v1:
time: 15.9 us; the launch traced here: 15.7 us
  Pallas kernels  15 us (94%)
  between operations  0.64 us (4%)
    pallas_call x1, Pallas kernels, shards(): pl.pallas_call(functools.partial(kernel, rows, cols), out_shape=(vmem((tr...  14.4 us
    pallas_call x1, Pallas kernels, shards(): pl.pallas_call(finish, out_shape=(jax.ShapeDtypeStruct((traits, own), f32...  0.62 us

profile of v1, /device:TPU:0, one launch (start us, length us, event | category | flops | bytes accessed | tf_op | source)
XLA Modules:
  0.0 15.7 jit_solution(4415269582871828477)
XLA Ops:
  0.6 14.4 %shard_map.41 = (f32[16,64]{1,0:T(8,128)S(1)}, f32[16,16]{1,0:T(8,128)S(1)}) custom-call(f32[16,64]{1,0:T(8,128)} %panel_hbm.1, f32[256,512]{1,0:T(8,128)} %kin_hbm.1), custom_call_target="tpu_custom_call" | custom-call | tf_op jit(solution)/shard_map/pallas_call | solution.py:395
  15.1 0.6 %shard_map.42 = (f32[16,64]{1,0:T(8,128)}, f32[16,16]{1,0:T(8,128)}) custom-call(f32[16,64]{1,0:T(8,128)S(1)} %get-tuple-element.4.value_ref, f32[16,16]{1,0:T(8,128)S(1)} %get-tuple-element.5.form_ref), custom_call_target="tpu_custom_call" | custom-call | tf_op jit(solution)/shard_map/pallas_call | solution.py:425
